TPU v7x, 256 devices: a 2x2x32 block of a 4x8x32 slice. The times are simulated.
256 devices in a mesh: parts: 4 (over y, x), dp: 64 (over z, core).
Axes of the slice: x: 2, y: 2, z: 32, core: 2. Of those that a mesh axis runs over, the one named last changes fastest.
The devices are a block of a 4x8x32 slice.
Arguments:
- activations: bfloat16 [65536, 14336], P(('parts', 'dp')), parts along dimension 0, may hold values from -6 to 6
- out_grads: bfloat16 [65536, 4096], P(('parts', 'dp')), parts along dimension 0, may hold values from -6 to 6
- lengths: int32 [256, 4], P(('parts', 'dp')), parts along dimension 0, may hold values from 1 to 128, 256 in all within a row
- proj_in: bfloat16 [14336, 64], replicated, may hold values from -0.046875 to 0.046875
- proj_out: bfloat16 [4096, 64], replicated, may hold values from -0.09375 to 0.09375
- queries: bfloat16 [8192, 4096], P(('parts', 'dp')), parts along dimension 0, may hold values from -0.01171875 to 0.01171875
Outputs:
- scores: bfloat16 [1024, 2048], P(('parts', 'dp')), parts along dimension 0
There are 4 independent parts, one for each index of `parts`. A program takes and returns all parts, laid end to end along the dimension named above; an argument that names none is the same for every part. Nothing has to cross between parts.
Inputs may be any that keep to these rules, and one draw needn't show every extreme that they name: Each row of lengths sums to 256, and one entry of each row equals 128.
All inputs are finite; a program needn't handle non-finite values.
Results may differ from a plain program's by a relative error of at most 0.0065.
Values may be sent and summed in bfloat16 or wider, within the bound.
A program may use at most 128 MiB of HBM per device.

v0:
```python
import jax
import jax.numpy as jnp
from jax import lax
from jax.sharding import PartitionSpec as P


def local(activations, out_grads, lengths, proj_in, proj_out, queries):
    tok_count = activations.shape[0]
    rank_size = proj_in.shape[1]
    proj_acts = jnp.dot(activations, proj_in, preferred_element_type=jnp.float32).astype(
        jnp.bfloat16
    )
    proj_grads = jnp.dot(out_grads, proj_out, preferred_element_type=jnp.float32).astype(
        jnp.bfloat16
    )
    counts = lengths[0]
    tok_ends = jnp.cumsum(counts)
    tok_starts = tok_ends - counts
    position = jnp.arange(tok_count, dtype=jnp.int32)
    member = (
        (position[None, :] >= tok_starts[:, None]) & (position[None, :] < tok_ends[:, None])
    ).astype(jnp.bfloat16)
    masked_grads = member[:, :, None] * proj_grads[None, :, :]
    summed = jnp.einsum("eti,tj->eij", masked_grads, proj_acts, preferred_element_type=jnp.float32)
    example_grads = summed.reshape(counts.shape[0], rank_size * rank_size).astype(jnp.bfloat16)
    contract = (((1,), (1,)), ((), ()))
    scores = lax.dot_general(
        example_grads,
        lax.all_gather(queries, "dp", axis=0, tiled=True),
        contract,
        preferred_element_type=jnp.float32,
    )
    return scores.astype(jnp.bfloat16)


def solution(mesh):
    in_specs = (
        P(("parts", "dp"), None),
        P(("parts", "dp"), None),
        P(("parts", "dp"), None),
        P(),
        P(),
        P(("parts", "dp"), None),
    )
    out_specs = P(("parts", "dp"), None)
    return jax.shard_map(local, mesh=mesh, in_specs=in_specs, out_specs=out_specs, check_vma=False)
```

profile of v0, /device:TPU:37, one launch (start us, length us, event | category | flops | bytes accessed | tf_op | source)
XLA Modules:
  0.0 188.2 jit_solution(3009798860218271106)
XLA Ops:
  6.5 0.0 copy-start
  6.6 0.0 all-gather.2.cloned.1.call-start
  6.6 0.7 all-gather.2.cloned.1.call-update
  7.3 0.8 reduce-window.7
  8.1 0.7 bitcast_subtract_fusion
  8.8 0.1 fusion.5
  8.9 0.0 copy-done
  8.9 1.8 convolution_convert_fusion.3
  10.7 6.2 %convolution_convert_fusion.1 = bf16[4,64,64]{2,1,0:T(8,128)(2,1)S(1)} fusion(bf16[256,14336]{1,0:T(8,128)(2,1)} %param.6, bf16[14336,64]{0,1:T(8,128)(2,1)} %param.9, bf16[256,64]{0,1:T(8,128)(2,1)S(1)} %convolution_convert_fusion.3, bf16[4,256]{1,0:T(4,128)(2,1)S(1)} %fusion.5), kind=kOutput, calls=%fused_computation.1 | convolution fusion | flops 478248960 | bytes 9242624 | tf_op jit(solution)/shard_map/eti,tj->eij/dot_general | solution.py:24
  16.9 0.1 convert_element_type.26
  17.0 153.5 %all-gather.2.cloned.1.call-done = bf16[2048,4096]{1,0:T(8,128)(2,1)} async-done(((bf16[32,4096]{1,0:T(8,128)(2,1)}), bf16[2048,4096]{1,0:T(8,128)(2,1)}) %all-gather.2.cloned.1.call-update) | async-done | bytes 16777232 | tf_op jit(solution)/shard_map/all_gather | solution.py:29
  170.5 10.8 %convolution_convert_fusion = bf16[4,2048]{1,0:T(4,128)(2,1)} fusion(bf16[4,4096]{1,0:T(4,128)(2,1)S(1)} %convert_element_type.26, bf16[2048,4096]{1,0:T(8,128)(2,1)} %all-gather.2.cloned.1.call-done), kind=kOutput, calls=%fused_computation | convolution fusion | flops 67117056 | bytes 16826368 | tf_op jit(solution)/shard_map/dot_general | solution.py:27
Async XLA Ops:
  6.5 2.3 %copy-start = (bf16[256,4096]{1,0:T(8,128)(2,1)S(1)}, bf16[256,4096]{1,0:T(8,128)(2,1)}, u32[]{:S(2)}) copy-start(bf16[256,4096]{1,0:T(8,128)(2,1)} %param.7) | copy-start | bytes 6291460
  6.6 163.9 %all-gather.2.cloned.1.call-start = ((), (), s32[]{:S(2)}) async-start(), calls=%async_computation | async-start | bytes 17039360 | tf_op jit(solution)/shard_map/all_gather | solution.py:29
Sparse Core Ops, SparseCore 0:
  9.2 161.2 all-gather.1
where the time goes:
time: 188 us
  waiting for transfers between devices  154 us (82%)
  matrix products  18.8 us (10%)
  between operations  13.4 us (7%)
    all_gather x1, waiting for transfers between devices, local(): lax.all_gather(queries, 'dp', axis=0, tiled=True)  153 us
    dot_general x1, matrix products, local(): lax.dot_general(example_grads, lax.all_gather(queries, 'dp', axis=0, tile...  10.8 us
    dot_general x1, matrix products, local(): jnp.einsum('eti,tj->eij', masked_grads, proj_acts, preferred_element_type...  6.21 us
  transfers between devices with their start and end apart: 1, of which 1 were waited for; matrix products, arithmetic and copies ran while one was open for 5% of the time, Pallas kernels for 0%

commit v1 on v0

--- a/solution.py
+++ b/solution.py
@@ -2,6 +2,17 @@
 import jax.numpy as jnp
 from jax import lax
 from jax.sharding import PartitionSpec as P
+
+
+def lay_positions(raw):
+    n_dev_all = lax.psum(1, axis_name="dp")
+    return lax.all_to_all(
+        jnp.tile(raw, tuple((n_dev_all if t == 0 else 1 for t in range(raw.ndim)))),
+        "dp",
+        split_axis=0,
+        concat_axis=0,
+        tiled=True,
+    )
 
 
 def local(activations, out_grads, lengths, proj_in, proj_out, queries):
@@ -25,10 +36,7 @@
     example_grads = summed.reshape(counts.shape[0], rank_size * rank_size).astype(jnp.bfloat16)
     contract = (((1,), (1,)), ((), ()))
     scores = lax.dot_general(
-        example_grads,
-        lax.all_gather(queries, "dp", axis=0, tiled=True),
-        contract,
-        preferred_element_type=jnp.float32,
+        example_grads, lay_positions(queries), contract, preferred_element_type=jnp.float32
     )
     return scores.astype(jnp.bfloat16)
 

time: 188 us -> 1510 us (8.03); the launches traced: 188 us -> 1490 us
  waiting for transfers between devices: 154 us -> 1430 us
  starting transfers between devices: 0.01 us -> 34.5 us
    all_to_all x0 -> x1, waiting for transfers between devices: none -> 1430 us  [lay_positions(): lax.all_to_all(jnp.tile(raw, tuple((n_dev_all if t == 0 else 1 for t in r...]
    all_gather x1 -> x0, waiting for transfers between devices: 153 us -> none  [local(): lax.all_gather(queries, 'dp', axis=0, tiled=True)]
    all_to_all x0 -> x1, starting transfers between devices: none -> 34.5 us  [lay_positions(): lax.all_to_all(jnp.tile(raw, tuple((n_dev_all if t == 0 else 1 for t in r...]
  transfers between devices with their start and end apart: 1 -> 1, of which waited for: 1 -> 1; matrix products, arithmetic and copies ran while one was open for 5% -> 0% of each run, Pallas kernels for 0% -> 0%
where the time goes in v1:
time: 1510 us; the launch traced here: 1490 us
  waiting for transfers between devices  1430 us (95%)
  starting transfers between devices  34.5 us (2%)
  matrix products  17.7 us (1%)
    all_to_all x1, waiting for transfers between devices, lay_positions(): lax.all_to_all(jnp.tile(raw, tuple((n_dev_all if t == 0 else 1 for t in r...  1430 us
    all_to_all x1, starting transfers between devices, lay_positions(): lax.all_to_all(jnp.tile(raw, tuple((n_dev_all if t == 0 else 1 for t in r...  34.5 us
  transfers between devices with their start and end apart: 1, of which 1 were waited for; matrix products, arithmetic and copies ran while one was open for 0% of the time, Pallas kernels for 0%

profile of v1, /device:TPU:37, one launch (start us, length us, event | category | flops | bytes accessed | tf_op | source)
XLA Modules:
  0.0 1486.6 jit_solution(3080879991786979918)
XLA Ops:
  0.0 0.0 copy-start
  0.0 6.9 tile.2
  6.9 0.0 copy-start.2
  6.9 0.0 copy-start.1
  6.9 34.5 %all-to-all-start = ((bf16[64,32,4096]{2,1,0:T(8,128)(2,1)}), bf16[64,32,4096]{2,1,0:T(8,128)(2,1)}, u32[]{:S(2)}, u32[]{:S(2)}) async-start(bf16[64,32,4096]{2,1,0:T(8,128)(2,1)} %tile.2), calls=%async_computation | async-start | bytes 33554432 | tf_op jit(solution)/shard_map/all_to_all | solution.py:9
  41.4 0.0 copy-done.2
  41.4 0.2 reduce-window.7
  41.6 0.1 fusion.5
  41.7 0.0 copy-done
  41.7 0.0 copy-done.1
  41.7 0.8 convolution_convert_fusion.3
  42.5 6.2 convolution_convert_fusion.1
  48.7 0.1 convert_element_type.26
  48.8 1427.0 %all-to-all-done = bf16[64,32,4096]{2,1,0:T(8,128)(2,1)} async-done(((bf16[64,32,4096]{2,1,0:T(8,128)(2,1)}), bf16[64,32,4096]{2,1,0:T(8,128)(2,1)}, u32[]{:S(2)}, u32[]{:S(2)}) %all-to-all-start) | async-done | bytes 16777248 | tf_op jit(solution)/shard_map/all_to_all | solution.py:9
  1475.8 10.8 convolution_convert_fusion
  (1 shorter events, 0.0 us)
Async XLA Ops:
  0.0 41.7 %copy-start = (bf16[256,4096]{1,0:T(8,128)(2,1)S(1)}, bf16[256,4096]{1,0:T(8,128)(2,1)}, u32[]{:S(2)}) copy-start(bf16[256,4096]{1,0:T(8,128)(2,1)} %param.7) | copy-start | bytes 6291460
  6.9 34.5 %copy-start.2 = (s32[1,4]{1,0:T(1,128)S(1)}, s32[1,4]{1,0:T(1,128)}, u32[]{:S(2)}) copy-start(s32[1,4]{1,0:T(1,128)} %param.8) | copy-start | bytes 52
  6.9 34.8 %copy-start.1 = (bf16[4096,64]{0,1:T(8,128)(2,1)S(1)}, bf16[4096,64]{0,1:T(8,128)(2,1)}, u32[]{:S(2)}) copy-start(bf16[4096,64]{0,1:T(8,128)(2,1)} %param.10) | copy-start | bytes 1572868
  6.9 1468.9 %all-to-all-start = ((bf16[64,32,4096]{2,1,0:T(8,128)(2,1)}), bf16[64,32,4096]{2,1,0:T(8,128)(2,1)}, u32[]{:S(2)}, u32[]{:S(2)}) async-start(bf16[64,32,4096]{2,1,0:T(8,128)(2,1)} %tile.2), calls=%async_computation | async-start | bytes 33554432 | tf_op jit(solution)/shard_map/all_to_all | solution.py:9
